TPU v7x, 32 devices: a whole 2x2x4 slice. The times are simulated.
32 devices in a mesh: pipe: 4 (over x, core), exp: 4 (over z), pair: 2 (over y).
Axes of the slice: x: 2, y: 2, z: 4, core: 2. Of those that a mesh axis runs over, the one named last changes fastest.
Arguments:
- hidden_in: bfloat16 [4, 256, 2048], P(None, ('exp', 'pair')), may hold values from -6 to 6
- routes: int32 [4, 4, 256, 8], P('pipe', None, ('exp', 'pair')), may hold values from 0 to 15, all different within a row; in each aligned block of 32 rows (0 to 31, 32 to 63, ..., all dimensions but the last counted through in order) at most 24 rows name the same one
- gate_probs: float32 [4, 4, 256, 8], P('pipe', None, ('exp', 'pair')), may hold values from 0.02 to 1
- norm_gain: float32 [4, 2048], P('pipe'), may hold values from 0.1 to 1.9
- w_gate: bfloat16 [4, 16, 2048, 768], P('pipe', ('exp', 'pair')), may hold values from -0.125 to 0.125
- w_up: bfloat16 [4, 16, 2048, 768], P('pipe', ('exp', 'pair')), may hold values from -0.125 to 0.125
- w_down: bfloat16 [4, 16, 768, 2048], P('pipe', ('exp', 'pair')), may hold values from -0.21875 to 0.21875
Outputs:
- layer_outputs: bfloat16 [4, 4, 256, 2048], P('pipe', None, ('exp', 'pair'))
Inputs may be any that keep to these rules, and one draw needn't show every extreme that they name: `routes`: within each layer and micro-batch, the 32 tokens of one device (aligned blocks) name no expert more than 24 times in all, and each token names 8 different experts.
All inputs are finite; a program needn't handle non-finite values.
Results may differ from a plain program's by a relative error of at most 0.01.
Values may be sent and summed in bfloat16 or wider, within the bound.
A program may use at most 64 MiB of HBM per device.

v0:
```python
import jax
import jax.numpy as jnp
from jax import lax
from jax.sharding import PartitionSpec as P

EPS = 1e-06


def passed_along(value, axis, steps):
    count = lax.axis_size(axis)
    first, last = (max(0, -steps), min(count, count - steps))
    return lax.ppermute(value, axis, [(source, source + steps) for source in range(first, last)])


def expert_block(arrived, wgate, wupper, wdown):
    gate = jnp.einsum("nlcd,ldf->nlcf", arrived, wgate, preferred_element_type=jnp.float32)
    upward = jnp.einsum("nlcd,ldf->nlcf", arrived, wupper, preferred_element_type=jnp.float32)
    hidden = (jax.nn.silu(gate) * upward).astype(jnp.bfloat16)
    return jnp.einsum("nlcf,lfd->nlcd", hidden, wdown, preferred_element_type=jnp.float32).astype(
        jnp.bfloat16
    )


def on_device(hidden_in, routes, gate_probs, norm_gain, w_gate, w_up, w_down):
    section = lax.axis_index("pipe")
    micro, tok_rows, width = hidden_in.shape
    top_count = routes.shape[3]
    groups = lax.axis_size(("exp", "pair"))
    local_experts = w_gate.shape[1]
    experts = local_experts * groups
    capacity = max(2, 3 * tok_rows * top_count // (2 * experts))
    gain = norm_gain[0]
    wgate = w_gate[0]
    wupper = w_up[0]
    wdown = w_down[0]
    expert_ids = jnp.arange(experts, dtype=jnp.int32)

    def layer(state, index):
        chosen = lax.dynamic_index_in_dim(routes[0], index, 0, keepdims=False).reshape(-1)
        probs = lax.dynamic_index_in_dim(gate_probs[0], index, 0, keepdims=False)
        floated = state.astype(jnp.float32)
        scale = lax.rsqrt(jnp.mean(floated * floated, axis=-1, keepdims=True) + EPS)
        normed = (floated * scale * gain).astype(jnp.bfloat16)
        onehot = (chosen[:, None] == expert_ids[None, :]).astype(jnp.int32)
        before = jnp.cumsum(onehot, axis=0) - onehot
        slots = jnp.sum(before * onehot, axis=1)
        outgoing = jnp.zeros((experts, capacity, width), jnp.bfloat16)
        outgoing = outgoing.at[chosen, slots].set(jnp.repeat(normed, top_count, axis=0))
        grouped = outgoing.reshape(groups, local_experts, capacity, width)
        produced = expert_block(
            lax.all_to_all(grouped, ("exp", "pair"), split_axis=0, concat_axis=0, tiled=True),
            wgate,
            wupper,
            wdown,
        )
        returned = lax.all_to_all(
            produced, ("exp", "pair"), split_axis=0, concat_axis=0, tiled=True
        )
        results = returned.reshape(experts, capacity, width)[chosen, slots]
        results = results.reshape(tok_rows, top_count, width).astype(jnp.float32)
        weights = probs / jnp.sum(probs, axis=-1, keepdims=True)
        mixed = jnp.einsum("tk,tkd->td", weights, results)
        return (floated + mixed).astype(jnp.bfloat16)

    def advance(step, carry):
        received, saved = carry
        index = step - section
        valid = jnp.logical_and(index >= 0, index < micro)
        clipped = jnp.clip(index, 0, micro - 1)
        first = lax.dynamic_index_in_dim(hidden_in, clipped, 0, keepdims=False)
        state = jnp.where(section == 0, first, received)
        updated = layer(state, clipped)
        saved = jnp.where(valid, lax.dynamic_update_index_in_dim(saved, updated, clipped, 0), saved)
        received = passed_along(updated, "pipe", 1)
        return (received, saved)

    start = (
        jnp.zeros((tok_rows, width), jnp.bfloat16),
        jnp.zeros((micro, tok_rows, width), jnp.bfloat16),
    )
    received, saved = lax.fori_loop(0, micro + lax.axis_size("pipe") - 1, advance, start)
    return saved[None]


def solution(mesh):
    in_specs = (
        P(None, ("exp", "pair"), None),
        P("pipe", None, ("exp", "pair"), None),
        P("pipe", None, ("exp", "pair"), None),
        P("pipe", None),
        P("pipe", ("exp", "pair"), None, None),
        P("pipe", ("exp", "pair"), None, None),
        P("pipe", ("exp", "pair"), None, None),
    )
    out_specs = P("pipe", None, ("exp", "pair"), None)
    return jax.shard_map(
        on_device, mesh=mesh, in_specs=in_specs, out_specs=out_specs, check_vma=False
    )
```

profile of v0, /device:TPU:1, one launch (start us, length us, event | category | flops | bytes accessed | tf_op | source)
XLA Modules:
  0.0 937.2 jit_solution(15736673222117613759)
XLA Ops:
  0.9 936.4 %while.18 = (s32[]{:T(128)}, bf16[32,2048]{1,0:T(8,128)(2,1)S(1)}, bf16[4,32,2048]{2,1,0:T(8,128)(2,1)}, pred[]{:T(512)}, s32[]{:T(128)}, /*index=5*/bf16[4,32,2...) while((s32[]{:T(128)}, bf16[32,2048]{1,0:T(8,128)(2,1)S(1)}, ...), condition=%wide.region_7.8_spmd.clone.clone, body=%wide.region_0.7_spmd.clone.clone.sunk | while | flops 3628826880 | bytes 48352280 | solution.py:81
  5.1 23.0 %scatter_fusion = bf16[16,24,2048]{2,1,0:T(8,128)(2,1)S(1)} fusion(bf16[16,24,2048]{2,1,0:T(8,128)(2,1)S(1)} %broadcast.269, s32[256]{0:T(256)S(1)} %bitcast.143, bf16[256,2048]{1,0:T(8,128)(2,1)S(1)} %broadcast_bitcast_fusion.2), kind=kCustom, calls=%fused_computation.1.clone.clone.1 | custom fusion | bytes 3147776 | tf_op jit(solution)/shard_map/while/body/eval_jaxpr/scatter | solution.py:48
  28.1 42.3 %all_to_all.26 = bf16[8,2,24,2048]{3,2,1,0:T(8,128)(2,1)S(1)} all-to-all(bf16[8,2,24,2048]{3,2,1,0:T(8,128)(2,1)S(1)} %bitcast.140), channel_id=1, replica_groups=mesh['pipe'=4,'exp'=4,'pair'=2] {'exp','pair'}, dimensions={0} | all-to-all | bytes 3145728 | tf_op jit(solution)/shard_map/while/body/eval_jaxpr/all_to_all | solution.py:51
  75.6 8.0 fusion.87
  89.2 35.8 %all-to-all-done.1 = bf16[8,2,24,2048]{3,2,1,0:T(8,128)(2,1)S(1)} async-done(((bf16[8,2,24,2048]{3,2,1,0:T(8,128)(2,1)}), bf16[8,2,24,2048]{3,2,1,0:T(8,128)(2,1)S(1)}, u32[]{:S(2)}, u32[]{:S(2)}) %all-to-all-start.1) | async-done | bytes 1572896 | tf_op jit(solution)/shard_map/while/body/eval_jaxpr/all_to_all | solution.py:56
  142.3 23.0 %scatter_fusion = bf16[16,24,2048]{2,1,0:T(8,128)(2,1)S(1)} fusion(bf16[16,24,2048]{2,1,0:T(8,128)(2,1)S(1)} %broadcast.269, s32[256]{0:T(256)S(1)} %bitcast.143, bf16[256,2048]{1,0:T(8,128)(2,1)S(1)} %broadcast_bitcast_fusion.2), kind=kCustom, calls=%fused_computation.1.clone.clone.1 | custom fusion | bytes 3147776 | tf_op jit(solution)/shard_map/while/body/eval_jaxpr/scatter | solution.py:48
  165.3 39.4 %all_to_all.26 = bf16[8,2,24,2048]{3,2,1,0:T(8,128)(2,1)S(1)} all-to-all(bf16[8,2,24,2048]{3,2,1,0:T(8,128)(2,1)S(1)} %bitcast.140), channel_id=1, replica_groups=mesh['pipe'=4,'exp'=4,'pair'=2] {'exp','pair'}, dimensions={0} | all-to-all | bytes 3145728 | tf_op jit(solution)/shard_map/while/body/eval_jaxpr/all_to_all | solution.py:51
  209.9 8.0 fusion.87
  223.0 36.4 %all-to-all-done.1 = bf16[8,2,24,2048]{3,2,1,0:T(8,128)(2,1)S(1)} async-done(((bf16[8,2,24,2048]{3,2,1,0:T(8,128)(2,1)}), bf16[8,2,24,2048]{3,2,1,0:T(8,128)(2,1)S(1)}, u32[]{:S(2)}, u32[]{:S(2)}) %all-to-all-start.1) | async-done | bytes 1572896 | tf_op jit(solution)/shard_map/while/body/eval_jaxpr/all_to_all | solution.py:56
  274.1 23.0 %scatter_fusion = bf16[16,24,2048]{2,1,0:T(8,128)(2,1)S(1)} fusion(bf16[16,24,2048]{2,1,0:T(8,128)(2,1)S(1)} %broadcast.269, s32[256]{0:T(256)S(1)} %bitcast.143, bf16[256,2048]{1,0:T(8,128)(2,1)S(1)} %broadcast_bitcast_fusion.2), kind=kCustom, calls=%fused_computation.1.clone.clone.1 | custom fusion | bytes 3147776 | tf_op jit(solution)/shard_map/while/body/eval_jaxpr/scatter | solution.py:48
  297.1 41.0 %all_to_all.26 = bf16[8,2,24,2048]{3,2,1,0:T(8,128)(2,1)S(1)} all-to-all(bf16[8,2,24,2048]{3,2,1,0:T(8,128)(2,1)S(1)} %bitcast.140), channel_id=1, replica_groups=mesh['pipe'=4,'exp'=4,'pair'=2] {'exp','pair'}, dimensions={0} | all-to-all | bytes 3145728 | tf_op jit(solution)/shard_map/while/body/eval_jaxpr/all_to_all | solution.py:51
  356.5 36.3 %all-to-all-done.1 = bf16[8,2,24,2048]{3,2,1,0:T(8,128)(2,1)S(1)} async-done(((bf16[8,2,24,2048]{3,2,1,0:T(8,128)(2,1)}), bf16[8,2,24,2048]{3,2,1,0:T(8,128)(2,1)S(1)}, u32[]{:S(2)}, u32[]{:S(2)}) %all-to-all-start.1) | async-done | bytes 1572896 | tf_op jit(solution)/shard_map/while/body/eval_jaxpr/all_to_all | solution.py:56
  407.2 23.0 %scatter_fusion = bf16[16,24,2048]{2,1,0:T(8,128)(2,1)S(1)} fusion(bf16[16,24,2048]{2,1,0:T(8,128)(2,1)S(1)} %broadcast.269, s32[256]{0:T(256)S(1)} %bitcast.143, bf16[256,2048]{1,0:T(8,128)(2,1)S(1)} %broadcast_bitcast_fusion.2), kind=kCustom, calls=%fused_computation.1.clone.clone.1 | custom fusion | bytes 3147776 | tf_op jit(solution)/shard_map/while/body/eval_jaxpr/scatter | solution.py:48
  430.2 41.4 %all_to_all.26 = bf16[8,2,24,2048]{3,2,1,0:T(8,128)(2,1)S(1)} all-to-all(bf16[8,2,24,2048]{3,2,1,0:T(8,128)(2,1)S(1)} %bitcast.140), channel_id=1, replica_groups=mesh['pipe'=4,'exp'=4,'pair'=2] {'exp','pair'}, dimensions={0} | all-to-all | bytes 3145728 | tf_op jit(solution)/shard_map/while/body/eval_jaxpr/all_to_all | solution.py:51
  490.0 36.1 %all-to-all-done.1 = bf16[8,2,24,2048]{3,2,1,0:T(8,128)(2,1)S(1)} async-done(((bf16[8,2,24,2048]{3,2,1,0:T(8,128)(2,1)}), bf16[8,2,24,2048]{3,2,1,0:T(8,128)(2,1)S(1)}, u32[]{:S(2)}, u32[]{:S(2)}) %all-to-all-start.1) | async-done | bytes 1572896 | tf_op jit(solution)/shard_map/while/body/eval_jaxpr/all_to_all | solution.py:56
  540.5 23.0 %scatter_fusion = bf16[16,24,2048]{2,1,0:T(8,128)(2,1)S(1)} fusion(bf16[16,24,2048]{2,1,0:T(8,128)(2,1)S(1)} %broadcast.269, s32[256]{0:T(256)S(1)} %bitcast.143, bf16[256,2048]{1,0:T(8,128)(2,1)S(1)} %broadcast_bitcast_fusion.2), kind=kCustom, calls=%fused_computation.1.clone.clone.1 | custom fusion | bytes 3147776 | tf_op jit(solution)/shard_map/while/body/eval_jaxpr/scatter | solution.py:48
  563.5 41.6 %all_to_all.26 = bf16[8,2,24,2048]{3,2,1,0:T(8,128)(2,1)S(1)} all-to-all(bf16[8,2,24,2048]{3,2,1,0:T(8,128)(2,1)S(1)} %bitcast.140), channel_id=1, replica_groups=mesh['pipe'=4,'exp'=4,'pair'=2] {'exp','pair'}, dimensions={0} | all-to-all | bytes 3145728 | tf_op jit(solution)/shard_map/while/body/eval_jaxpr/all_to_all | solution.py:51
  623.5 36.3 %all-to-all-done.1 = bf16[8,2,24,2048]{3,2,1,0:T(8,128)(2,1)S(1)} async-done(((bf16[8,2,24,2048]{3,2,1,0:T(8,128)(2,1)}), bf16[8,2,24,2048]{3,2,1,0:T(8,128)(2,1)S(1)}, u32[]{:S(2)}, u32[]{:S(2)}) %all-to-all-start.1) | async-done | bytes 1572896 | tf_op jit(solution)/shard_map/while/body/eval_jaxpr/all_to_all | solution.py:56
  674.2 23.0 %scatter_fusion = bf16[16,24,2048]{2,1,0:T(8,128)(2,1)S(1)} fusion(bf16[16,24,2048]{2,1,0:T(8,128)(2,1)S(1)} %broadcast.269, s32[256]{0:T(256)S(1)} %bitcast.143, bf16[256,2048]{1,0:T(8,128)(2,1)S(1)} %broadcast_bitcast_fusion.2), kind=kCustom, calls=%fused_computation.1.clone.clone.1 | custom fusion | bytes 3147776 | tf_op jit(solution)/shard_map/while/body/eval_jaxpr/scatter | solution.py:48
  697.3 41.4 %all_to_all.26 = bf16[8,2,24,2048]{3,2,1,0:T(8,128)(2,1)S(1)} all-to-all(bf16[8,2,24,2048]{3,2,1,0:T(8,128)(2,1)S(1)} %bitcast.140), channel_id=1, replica_groups=mesh['pipe'=4,'exp'=4,'pair'=2] {'exp','pair'}, dimensions={0} | all-to-all | bytes 3145728 | tf_op jit(solution)/shard_map/while/body/eval_jaxpr/all_to_all | solution.py:51
  757.1 36.3 %all-to-all-done.1 = bf16[8,2,24,2048]{3,2,1,0:T(8,128)(2,1)S(1)} async-done(((bf16[8,2,24,2048]{3,2,1,0:T(8,128)(2,1)}), bf16[8,2,24,2048]{3,2,1,0:T(8,128)(2,1)S(1)}, u32[]{:S(2)}, u32[]{:S(2)}) %all-to-all-start.1) | async-done | bytes 1572896 | tf_op jit(solution)/shard_map/while/body/eval_jaxpr/all_to_all | solution.py:56
  807.8 23.0 %scatter_fusion = bf16[16,24,2048]{2,1,0:T(8,128)(2,1)S(1)} fusion(bf16[16,24,2048]{2,1,0:T(8,128)(2,1)S(1)} %broadcast.269, s32[256]{0:T(256)S(1)} %bitcast.143, bf16[256,2048]{1,0:T(8,128)(2,1)S(1)} %broadcast_bitcast_fusion.2), kind=kCustom, calls=%fused_computation.1.clone.clone.1 | custom fusion | bytes 3147776 | tf_op jit(solution)/shard_map/while/body/eval_jaxpr/scatter | solution.py:48
  830.8 41.4 %all_to_all.26 = bf16[8,2,24,2048]{3,2,1,0:T(8,128)(2,1)S(1)} all-to-all(bf16[8,2,24,2048]{3,2,1,0:T(8,128)(2,1)S(1)} %bitcast.140), channel_id=1, replica_groups=mesh['pipe'=4,'exp'=4,'pair'=2] {'exp','pair'}, dimensions={0} | all-to-all | bytes 3145728 | tf_op jit(solution)/shard_map/while/body/eval_jaxpr/all_to_all | solution.py:51
  890.6 36.3 %all-to-all-done.1 = bf16[8,2,24,2048]{3,2,1,0:T(8,128)(2,1)S(1)} async-done(((bf16[8,2,24,2048]{3,2,1,0:T(8,128)(2,1)}), bf16[8,2,24,2048]{3,2,1,0:T(8,128)(2,1)S(1)}, u32[]{:S(2)}, u32[]{:S(2)}) %all-to-all-start.1) | async-done | bytes 1572896 | tf_op jit(solution)/shard_map/while/body/eval_jaxpr/all_to_all | solution.py:56
  (217 shorter events, 217.5 us)
Async XLA Ops:
  84.8 4.3 copy-start
  84.8 40.2 %all-to-all-start.1 = ((bf16[8,2,24,2048]{3,2,1,0:T(8,128)(2,1)}), bf16[8,2,24,2048]{3,2,1,0:T(8,128)(2,1)S(1)}, u32[]{:S(2)}, u32[]{:S(2)}) async-start(bf16[8,2,24,2048]{3,2,1,0:T(8,128)(2,1)} %copy.47), calls=%async_computation.1 | async-start | bytes 3145728 | tf_op jit(solution)/shard_map/while/body/eval_jaxpr/all_to_all | solution.py:56
  131.5 6.6 collective-permute-start
  219.1 3.7 copy-start
  219.1 40.2 %all-to-all-start.1 = ((bf16[8,2,24,2048]{3,2,1,0:T(8,128)(2,1)}), bf16[8,2,24,2048]{3,2,1,0:T(8,128)(2,1)S(1)}, u32[]{:S(2)}, u32[]{:S(2)}) async-start(bf16[8,2,24,2048]{3,2,1,0:T(8,128)(2,1)} %copy.47), calls=%async_computation.1 | async-start | bytes 3145728 | tf_op jit(solution)/shard_map/while/body/eval_jaxpr/all_to_all | solution.py:56
  265.8 4.1 collective-permute-start
  352.5 3.8 copy-start
  352.5 40.2 %all-to-all-start.1 = ((bf16[8,2,24,2048]{3,2,1,0:T(8,128)(2,1)}), bf16[8,2,24,2048]{3,2,1,0:T(8,128)(2,1)S(1)}, u32[]{:S(2)}, u32[]{:S(2)}) async-start(bf16[8,2,24,2048]{3,2,1,0:T(8,128)(2,1)} %copy.47), calls=%async_computation.1 | async-start | bytes 3145728 | tf_op jit(solution)/shard_map/while/body/eval_jaxpr/all_to_all | solution.py:56
  399.2 3.8 collective-permute-start
  486.1 3.7 copy-start
  486.1 39.9 %all-to-all-start.1 = ((bf16[8,2,24,2048]{3,2,1,0:T(8,128)(2,1)}), bf16[8,2,24,2048]{3,2,1,0:T(8,128)(2,1)S(1)}, u32[]{:S(2)}, u32[]{:S(2)}) async-start(bf16[8,2,24,2048]{3,2,1,0:T(8,128)(2,1)} %copy.47), calls=%async_computation.1 | async-start | bytes 3145728 | tf_op jit(solution)/shard_map/while/body/eval_jaxpr/all_to_all | solution.py:56
  532.5 3.8 collective-permute-start
  619.5 3.8 copy-start
  619.5 40.2 %all-to-all-start.1 = ((bf16[8,2,24,2048]{3,2,1,0:T(8,128)(2,1)}), bf16[8,2,24,2048]{3,2,1,0:T(8,128)(2,1)S(1)}, u32[]{:S(2)}, u32[]{:S(2)}) async-start(bf16[8,2,24,2048]{3,2,1,0:T(8,128)(2,1)} %copy.47), calls=%async_computation.1 | async-start | bytes 3145728 | tf_op jit(solution)/shard_map/while/body/eval_jaxpr/all_to_all | solution.py:56
  666.2 3.8 collective-permute-start
  753.1 3.8 copy-start
  753.1 40.2 %all-to-all-start.1 = ((bf16[8,2,24,2048]{3,2,1,0:T(8,128)(2,1)}), bf16[8,2,24,2048]{3,2,1,0:T(8,128)(2,1)S(1)}, u32[]{:S(2)}, u32[]{:S(2)}) async-start(bf16[8,2,24,2048]{3,2,1,0:T(8,128)(2,1)} %copy.47), calls=%async_computation.1 | async-start | bytes 3145728 | tf_op jit(solution)/shard_map/while/body/eval_jaxpr/all_to_all | solution.py:56
  799.8 3.8 collective-permute-start
  886.7 3.8 copy-start
  886.7 40.2 %all-to-all-start.1 = ((bf16[8,2,24,2048]{3,2,1,0:T(8,128)(2,1)}), bf16[8,2,24,2048]{3,2,1,0:T(8,128)(2,1)S(1)}, u32[]{:S(2)}, u32[]{:S(2)}) async-start(bf16[8,2,24,2048]{3,2,1,0:T(8,128)(2,1)} %copy.47), calls=%async_computation.1 | async-start | bytes 3145728 | tf_op jit(solution)/shard_map/while/body/eval_jaxpr/all_to_all | solution.py:56
  933.4 3.8 collective-permute-start
where the time goes:
time: 940 us; the launch traced here: 937 us
  blocking collectives  289 us (31%)
  waiting for transfers between devices  267 us (28%)
  local copies, waits for them, and re-layouts  212 us (23%)
  matrix products  95.1 us (10%)
  starting transfers between devices  43.2 us (5%)
  other arithmetic  30.3 us (3%)
    all_to_all x7, blocking collectives, layer(): lax.all_to_all(grouped, ('exp', 'pair'), split_axis=0, concat_axis=0, til...  289 us
    all_to_all x7, waiting for transfers between devices, layer(): lax.all_to_all(produced, ('exp', 'pair'), split_axis=0, concat_axis=0, ti...  253 us
    scatter x7, local copies, waits for them, and re-layouts, layer(): outgoing.at[chosen, slots].set(jnp.repeat(normed, top_count, axis=0))  161 us
    dot_general x7, matrix products, expert_block(): jnp.einsum('nlcf,lfd->nlcd', hidden, wdown, preferred_element_type=jnp.fl...  55.9 us
    dot_general x7, matrix products, expert_block(): jnp.einsum('nlcd,ldf->nlcf', arrived, wgate, preferred_element_type=jnp.f...  36.3 us
    gather x7, local copies, waits for them, and re-layouts, layer(): results = returned.reshape(experts, capacity, width)[chosen, slots]  30.3 us
    all_to_all x7, starting transfers between devices, layer(): lax.all_to_all(produced, ('exp', 'pair'), split_axis=0, concat_axis=0, ti...  26.8 us
  transfers between devices with their start and end apart: 14, of which 14 were waited for; matrix products, arithmetic and copies ran while one was open for 0% of the time, Pallas kernels for 0%

commit v1 on v0

--- a/solution.py
+++ b/solution.py
@@ -4,6 +4,29 @@
 from jax.sharding import PartitionSpec as P
 
 EPS = 1e-06
+
+
+def split_up(x, dim, length):
+    before, after = (x.shape[:dim], x.shape[dim + 1 :])
+    return jnp.moveaxis(x.reshape(*before, length, -1, *after), dim, 0)
+
+
+def joined_along(blocks, dim):
+    blocks = jnp.moveaxis(blocks, 0, dim)
+    lengths = blocks.shape
+    return blocks.reshape(*lengths[:dim], lengths[dim] * lengths[dim + 1], *lengths[dim + 2 :])
+
+
+def sent_to_each(x, axis, split_dim, concat_dim):
+    size, position = (lax.axis_size(axis), lax.axis_index(axis))
+    tiles = split_up(x, split_dim, size)
+    out = tiles
+    for step in range(1, size):
+        target, source = ((position + step) % size, (position - step) % size)
+        sent = lax.dynamic_index_in_dim(tiles, target, 0)
+        other = lax.ppermute(sent, axis, [(i, (i + step) % size) for i in range(size)])
+        out = lax.dynamic_update_slice_in_dim(out, other, source, axis=0)
+    return joined_along(out, concat_dim)
 
 
 def passed_along(value, axis, steps):
@@ -47,12 +70,7 @@
         outgoing = jnp.zeros((experts, capacity, width), jnp.bfloat16)
         outgoing = outgoing.at[chosen, slots].set(jnp.repeat(normed, top_count, axis=0))
         grouped = outgoing.reshape(groups, local_experts, capacity, width)
-        produced = expert_block(
-            lax.all_to_all(grouped, ("exp", "pair"), split_axis=0, concat_axis=0, tiled=True),
-            wgate,
-            wupper,
-            wdown,
-        )
+        produced = expert_block(sent_to_each(grouped, ("exp", "pair"), 0, 0), wgate, wupper, wdown)
         returned = lax.all_to_all(
             produced, ("exp", "pair"), split_axis=0, concat_axis=0, tiled=True
         )

time: 940 us -> 923 us (0.982)
  blocking collectives: 289 us -> 0 us
  starting transfers between devices: 43.2 us -> 202 us
  waiting for transfers between devices: 267 us -> 358 us
  local copies, waits for them, and re-layouts: 212 us -> 234 us
    all_to_all x7 -> x0, blocking collectives: 289 us -> none  [layer(): lax.all_to_all(grouped, ('exp', 'pair'), split_axis=0, concat_axis=0, til...]
    ppermute x0 -> x49, waiting for transfers between devices: none -> 91.7 us  [sent_to_each(): lax.ppermute(sent, axis, [(i, (i + step) % size) for i in range(size)])]
    all_to_all x7, starting transfers between devices: 26.8 us -> 102 us  [layer(): lax.all_to_all(produced, ('exp', 'pair'), split_axis=0, concat_axis=0, ti...]
    ppermute x0 -> x49, starting transfers between devices: none -> 74.1 us  [sent_to_each(): lax.ppermute(sent, axis, [(i, (i + step) % size) for i in range(size)])]
    dynamic_update_slice x0 -> x49, local copies, waits for them, and re-layouts: none -> 20.3 us  [sent_to_each(): out = lax.dynamic_update_slice_in_dim(out, other, source, axis=0)]
    ppermute x7, starting transfers between devices: 16.4 us -> 25.8 us  [passed_along(): lax.ppermute(value, axis, [(source, source + steps) for source in range(f...]
  transfers between devices with their start and end apart: 14 -> 63, of which waited for: 14 -> 28; matrix products, arithmetic and copies ran while one was open for 0% -> 2% of each run, Pallas kernels for 0% -> 0%
where the time goes in v1:
time: 923 us; the launch traced here: 921 us
  waiting for transfers between devices  358 us (39%)
  local copies, waits for them, and re-layouts  234 us (25%)
  starting transfers between devices  202 us (22%)
  matrix products  95.1 us (10%)
  other arithmetic  30.3 us (3%)
    all_to_all x7, waiting for transfers between devices, layer(): lax.all_to_all(produced, ('exp', 'pair'), split_axis=0, concat_axis=0, ti...  253 us
    scatter x7, local copies, waits for them, and re-layouts, layer(): outgoing.at[chosen, slots].set(jnp.repeat(normed, top_count, axis=0))  161 us
    all_to_all x7, starting transfers between devices, layer(): lax.all_to_all(produced, ('exp', 'pair'), split_axis=0, concat_axis=0, ti...  102 us
    ppermute x49, waiting for transfers between devices, sent_to_each(): lax.ppermute(sent, axis, [(i, (i + step) % size) for i in range(size)])  91.7 us
    ppermute x49, starting transfers between devices, sent_to_each(): lax.ppermute(sent, axis, [(i, (i + step) % size) for i in range(size)])  74.1 us
    dot_general x7, matrix products, expert_block(): jnp.einsum('nlcf,lfd->nlcd', hidden, wdown, preferred_element_type=jnp.fl...  55.9 us
    dot_general x7, matrix products, expert_block(): jnp.einsum('nlcd,ldf->nlcf', arrived, wgate, preferred_element_type=jnp.f...  36.3 us
    gather x7, local copies, waits for them, and re-layouts, layer(): results = returned.reshape(experts, capacity, width)[chosen, slots]  30.3 us
  transfers between devices with their start and end apart: 63, of which 28 were waited for; matrix products, arithmetic and copies ran while one was open for 2% of the time, Pallas kernels for 0%

profile of v1, /device:TPU:1, one launch (start us, length us, event | category | flops | bytes accessed | tf_op | source)
XLA Modules:
  0.0 920.6 jit_solution(4657717533576197523)
XLA Ops:
  0.9 919.7 %while.19 = (s32[]{:T(128)}, bf16[32,2048]{1,0:T(8,128)(2,1)S(1)}, bf16[4,32,2048]{2,1,0:T(8,128)(2,1)}, pred[]{:T(512)}, s32[]{:T(128)}, /*index=5*/bf16[4,32,2...) while((s32[]{:T(128)}, bf16[32,2048]{1,0:T(8,128)(2,1)S(1)}, ...), condition=%wide.region_7.8_spmd.clone.clone, body=%wide.region_0.7_spmd.clone.clone.sunk | while | flops 3628827136 | bytes 56219292 | solution.py:99
  5.2 23.0 %scatter_fusion = bf16[16,24,2048]{2,1,0:T(8,128)(2,1)S(1)} fusion(bf16[16,24,2048]{2,1,0:T(8,128)(2,1)S(1)} %broadcast.309, s32[256]{0:T(256)S(1)} %bitcast.171, bf16[256,2048]{1,0:T(8,128)(2,1)S(1)} %broadcast_bitcast_fusion.2), kind=kCustom, calls=%fused_computation.1.clone.clone.1 | custom fusion | bytes 3147776 | tf_op jit(solution)/shard_map/while/body/eval_jaxpr/scatter | solution.py:71
  44.5 11.4 %collective-permute-done.2 = bf16[1,1,2,24,2048]{4,3,2,1,0:T(8,128)(2,1)} collective-permute-done((bf16[1,1,2,24,2048]{4,3,2,1,0:T(8,128)(2,1)S(1)}, bf16[1,1,2,24,2048]{4,3,2,1,0:T(8,128)(2,1)}, u32[]{:S(2)}, u32[]{:S(2)}) %collective-permute-start.2) | collective-permute-done | bytes 196640 | tf_op jit(solution)/shard_map/while/body/eval_jaxpr/ppermute | solution.py:27
  71.5 14.3 %all-to-all-start = ((bf16[8,2,24,2048]{3,2,1,0:T(8,128)(2,1)}), bf16[8,2,24,2048]{3,2,1,0:T(8,128)(2,1)S(1)}, u32[]{:S(2)}, u32[]{:S(2)}) async-start(bf16[8,2,24,2048]{3,2,1,0:T(8,128)(2,1)} %copy.53), calls=%async_computation | async-start | bytes 3145728 | tf_op jit(solution)/shard_map/while/body/eval_jaxpr/all_to_all | solution.py:74
  85.9 35.0 %all-to-all-done = bf16[8,2,24,2048]{3,2,1,0:T(8,128)(2,1)S(1)} async-done(((bf16[8,2,24,2048]{3,2,1,0:T(8,128)(2,1)}), bf16[8,2,24,2048]{3,2,1,0:T(8,128)(2,1)S(1)}, u32[]{:S(2)}, u32[]{:S(2)}) %all-to-all-start) | async-done | bytes 1572896 | tf_op jit(solution)/shard_map/while/body/eval_jaxpr/all_to_all | solution.py:74
  139.4 23.0 %scatter_fusion = bf16[16,24,2048]{2,1,0:T(8,128)(2,1)S(1)} fusion(bf16[16,24,2048]{2,1,0:T(8,128)(2,1)S(1)} %broadcast.309, s32[256]{0:T(256)S(1)} %bitcast.171, bf16[256,2048]{1,0:T(8,128)(2,1)S(1)} %broadcast_bitcast_fusion.2), kind=kCustom, calls=%fused_computation.1.clone.clone.1 | custom fusion | bytes 3147776 | tf_op jit(solution)/shard_map/while/body/eval_jaxpr/scatter | solution.py:71
  176.7 10.2 %collective-permute-done.2 = bf16[1,1,2,24,2048]{4,3,2,1,0:T(8,128)(2,1)} collective-permute-done((bf16[1,1,2,24,2048]{4,3,2,1,0:T(8,128)(2,1)S(1)}, bf16[1,1,2,24,2048]{4,3,2,1,0:T(8,128)(2,1)}, u32[]{:S(2)}, u32[]{:S(2)}) %collective-permute-start.2) | collective-permute-done | bytes 196640 | tf_op jit(solution)/shard_map/while/body/eval_jaxpr/ppermute | solution.py:27
  202.5 14.4 %all-to-all-start = ((bf16[8,2,24,2048]{3,2,1,0:T(8,128)(2,1)}), bf16[8,2,24,2048]{3,2,1,0:T(8,128)(2,1)S(1)}, u32[]{:S(2)}, u32[]{:S(2)}) async-start(bf16[8,2,24,2048]{3,2,1,0:T(8,128)(2,1)} %copy.53), calls=%async_computation | async-start | bytes 3145728 | tf_op jit(solution)/shard_map/while/body/eval_jaxpr/all_to_all | solution.py:74
  217.1 36.3 %all-to-all-done = bf16[8,2,24,2048]{3,2,1,0:T(8,128)(2,1)S(1)} async-done(((bf16[8,2,24,2048]{3,2,1,0:T(8,128)(2,1)}), bf16[8,2,24,2048]{3,2,1,0:T(8,128)(2,1)S(1)}, u32[]{:S(2)}, u32[]{:S(2)}) %all-to-all-start) | async-done | bytes 1572896 | tf_op jit(solution)/shard_map/while/body/eval_jaxpr/all_to_all | solution.py:74
  270.2 23.0 %scatter_fusion = bf16[16,24,2048]{2,1,0:T(8,128)(2,1)S(1)} fusion(bf16[16,24,2048]{2,1,0:T(8,128)(2,1)S(1)} %broadcast.309, s32[256]{0:T(256)S(1)} %bitcast.171, bf16[256,2048]{1,0:T(8,128)(2,1)S(1)} %broadcast_bitcast_fusion.2), kind=kCustom, calls=%fused_computation.1.clone.clone.1 | custom fusion | bytes 3147776 | tf_op jit(solution)/shard_map/while/body/eval_jaxpr/scatter | solution.py:71
  333.6 14.6 %all-to-all-start = ((bf16[8,2,24,2048]{3,2,1,0:T(8,128)(2,1)}), bf16[8,2,24,2048]{3,2,1,0:T(8,128)(2,1)S(1)}, u32[]{:S(2)}, u32[]{:S(2)}) async-start(bf16[8,2,24,2048]{3,2,1,0:T(8,128)(2,1)} %copy.53), calls=%async_computation | async-start | bytes 3145728 | tf_op jit(solution)/shard_map/while/body/eval_jaxpr/all_to_all | solution.py:74
  348.3 36.3 %all-to-all-done = bf16[8,2,24,2048]{3,2,1,0:T(8,128)(2,1)S(1)} async-done(((bf16[8,2,24,2048]{3,2,1,0:T(8,128)(2,1)}), bf16[8,2,24,2048]{3,2,1,0:T(8,128)(2,1)S(1)}, u32[]{:S(2)}, u32[]{:S(2)}) %all-to-all-start) | async-done | bytes 1572896 | tf_op jit(solution)/shard_map/while/body/eval_jaxpr/all_to_all | solution.py:74
  401.1 23.0 %scatter_fusion = bf16[16,24,2048]{2,1,0:T(8,128)(2,1)S(1)} fusion(bf16[16,24,2048]{2,1,0:T(8,128)(2,1)S(1)} %broadcast.309, s32[256]{0:T(256)S(1)} %bitcast.171, bf16[256,2048]{1,0:T(8,128)(2,1)S(1)} %broadcast_bitcast_fusion.2), kind=kCustom, calls=%fused_computation.1.clone.clone.1 | custom fusion | bytes 3147776 | tf_op jit(solution)/shard_map/while/body/eval_jaxpr/scatter | solution.py:71
  464.8 14.7 %all-to-all-start = ((bf16[8,2,24,2048]{3,2,1,0:T(8,128)(2,1)}), bf16[8,2,24,2048]{3,2,1,0:T(8,128)(2,1)S(1)}, u32[]{:S(2)}, u32[]{:S(2)}) async-start(bf16[8,2,24,2048]{3,2,1,0:T(8,128)(2,1)} %copy.53), calls=%async_computation | async-start | bytes 3145728 | tf_op jit(solution)/shard_map/while/body/eval_jaxpr/all_to_all | solution.py:74
  479.7 36.3 %all-to-all-done = bf16[8,2,24,2048]{3,2,1,0:T(8,128)(2,1)S(1)} async-done(((bf16[8,2,24,2048]{3,2,1,0:T(8,128)(2,1)}), bf16[8,2,24,2048]{3,2,1,0:T(8,128)(2,1)S(1)}, u32[]{:S(2)}, u32[]{:S(2)}) %all-to-all-start) | async-done | bytes 1572896 | tf_op jit(solution)/shard_map/while/body/eval_jaxpr/all_to_all | solution.py:74
  532.0 23.0 %scatter_fusion = bf16[16,24,2048]{2,1,0:T(8,128)(2,1)S(1)} fusion(bf16[16,24,2048]{2,1,0:T(8,128)(2,1)S(1)} %broadcast.309, s32[256]{0:T(256)S(1)} %bitcast.171, bf16[256,2048]{1,0:T(8,128)(2,1)S(1)} %broadcast_bitcast_fusion.2), kind=kCustom, calls=%fused_computation.1.clone.clone.1 | custom fusion | bytes 3147776 | tf_op jit(solution)/shard_map/while/body/eval_jaxpr/scatter | solution.py:71
  596.2 14.6 %all-to-all-start = ((bf16[8,2,24,2048]{3,2,1,0:T(8,128)(2,1)}), bf16[8,2,24,2048]{3,2,1,0:T(8,128)(2,1)S(1)}, u32[]{:S(2)}, u32[]{:S(2)}) async-start(bf16[8,2,24,2048]{3,2,1,0:T(8,128)(2,1)} %copy.53), calls=%async_computation | async-start | bytes 3145728 | tf_op jit(solution)/shard_map/while/body/eval_jaxpr/all_to_all | solution.py:74
  610.9 36.3 %all-to-all-done = bf16[8,2,24,2048]{3,2,1,0:T(8,128)(2,1)S(1)} async-done(((bf16[8,2,24,2048]{3,2,1,0:T(8,128)(2,1)}), bf16[8,2,24,2048]{3,2,1,0:T(8,128)(2,1)S(1)}, u32[]{:S(2)}, u32[]{:S(2)}) %all-to-all-start) | async-done | bytes 1572896 | tf_op jit(solution)/shard_map/while/body/eval_jaxpr/all_to_all | solution.py:74
  662.9 23.0 %scatter_fusion = bf16[16,24,2048]{2,1,0:T(8,128)(2,1)S(1)} fusion(bf16[16,24,2048]{2,1,0:T(8,128)(2,1)S(1)} %broadcast.309, s32[256]{0:T(256)S(1)} %bitcast.171, bf16[256,2048]{1,0:T(8,128)(2,1)S(1)} %broadcast_bitcast_fusion.2), kind=kCustom, calls=%fused_computation.1.clone.clone.1 | custom fusion | bytes 3147776 | tf_op jit(solution)/shard_map/while/body/eval_jaxpr/scatter | solution.py:71
  727.5 14.6 %all-to-all-start = ((bf16[8,2,24,2048]{3,2,1,0:T(8,128)(2,1)}), bf16[8,2,24,2048]{3,2,1,0:T(8,128)(2,1)S(1)}, u32[]{:S(2)}, u32[]{:S(2)}) async-start(bf16[8,2,24,2048]{3,2,1,0:T(8,128)(2,1)} %copy.53), calls=%async_computation | async-start | bytes 3145728 | tf_op jit(solution)/shard_map/while/body/eval_jaxpr/all_to_all | solution.py:74
  742.2 36.3 %all-to-all-done = bf16[8,2,24,2048]{3,2,1,0:T(8,128)(2,1)S(1)} async-done(((bf16[8,2,24,2048]{3,2,1,0:T(8,128)(2,1)}), bf16[8,2,24,2048]{3,2,1,0:T(8,128)(2,1)S(1)}, u32[]{:S(2)}, u32[]{:S(2)}) %all-to-all-start) | async-done | bytes 1572896 | tf_op jit(solution)/shard_map/while/body/eval_jaxpr/all_to_all | solution.py:74
  793.9 23.0 %scatter_fusion = bf16[16,24,2048]{2,1,0:T(8,128)(2,1)S(1)} fusion(bf16[16,24,2048]{2,1,0:T(8,128)(2,1)S(1)} %broadcast.309, s32[256]{0:T(256)S(1)} %bitcast.171, bf16[256,2048]{1,0:T(8,128)(2,1)S(1)} %broadcast_bitcast_fusion.2), kind=kCustom, calls=%fused_computation.1.clone.clone.1 | custom fusion | bytes 3147776 | tf_op jit(solution)/shard_map/while/body/eval_jaxpr/scatter | solution.py:71
  858.8 14.5 %all-to-all-start = ((bf16[8,2,24,2048]{3,2,1,0:T(8,128)(2,1)}), bf16[8,2,24,2048]{3,2,1,0:T(8,128)(2,1)S(1)}, u32[]{:S(2)}, u32[]{:S(2)}) async-start(bf16[8,2,24,2048]{3,2,1,0:T(8,128)(2,1)} %copy.53), calls=%async_computation | async-start | bytes 3145728 | tf_op jit(solution)/shard_map/while/body/eval_jaxpr/all_to_all | solution.py:74
  873.4 36.2 %all-to-all-done = bf16[8,2,24,2048]{3,2,1,0:T(8,128)(2,1)S(1)} async-done(((bf16[8,2,24,2048]{3,2,1,0:T(8,128)(2,1)}), bf16[8,2,24,2048]{3,2,1,0:T(8,128)(2,1)S(1)}, u32[]{:S(2)}, u32[]{:S(2)}) %all-to-all-start) | async-done | bytes 1572896 | tf_op jit(solution)/shard_map/while/body/eval_jaxpr/all_to_all | solution.py:74
  (364 shorter events, 381.7 us)
Async XLA Ops:
  31.8 24.1 %collective-permute-start.2 = (bf16[1,1,2,24,2048]{4,3,2,1,0:T(8,128)(2,1)S(1)}, bf16[1,1,2,24,2048]{4,3,2,1,0:T(8,128)(2,1)}, u32[]{:S(2)}, u32[]{:S(2)}) collective-permute-start(bf16[1,1,2,24,2048]{4,3,2,1,0:T(8,128)(2,1)S(1)} %get-tuple-element.529), channel_id=1, source_target_pairs={{0,3},{1,4},{2,5},{3,6},{4,7},{5,0},{6,1},{7,2},{8,11},{9,12},{10,... | collective-permute-start | bytes 589832 | tf_op jit(solution)/shard_map/while/body/eval_jaxpr/ppermute | solution.py:27
  34.0 22.8 %collective-permute-start.3 = (bf16[1,1,2,24,2048]{4,3,2,1,0:T(8,128)(2,1)S(1)}, bf16[1,1,2,24,2048]{4,3,2,1,0:T(8,128)(2,1)S(1)}, u32[]{:S(2)}, u32[]{:S(2)}) collective-permute-start(bf16[1,1,2,24,2048]{4,3,2,1,0:T(8,128)(2,1)S(1)} %get-tuple-element.530), channel_id=1, source_target_pairs={{0,4},{1,5},{2,6},{3,7},{4,0},{5,1},{6,2},{7,3},{8,12},{9,13},{10,... | collective-permute-start | bytes 589832 | tf_op jit(solution)/shard_map/while/body/eval_jaxpr/ppermute | solution.py:27
  35.0 21.9 %collective-permute-start.4 = (bf16[1,1,2,24,2048]{4,3,2,1,0:T(8,128)(2,1)S(1)}, bf16[1,1,2,24,2048]{4,3,2,1,0:T(8,128)(2,1)S(1)}, u32[]{:S(2)}, u32[]{:S(2)}) collective-permute-start(bf16[1,1,2,24,2048]{4,3,2,1,0:T(8,128)(2,1)S(1)} %get-tuple-element.531), channel_id=1, source_target_pairs={{0,5},{1,6},{2,7},{3,0},{4,1},{5,2},{6,3},{7,4},{8,13},{9,14},{10,... | collective-permute-start | bytes 589832 | tf_op jit(solution)/shard_map/while/body/eval_jaxpr/ppermute | solution.py:27
  71.5 49.4 %all-to-all-start = ((bf16[8,2,24,2048]{3,2,1,0:T(8,128)(2,1)}), bf16[8,2,24,2048]{3,2,1,0:T(8,128)(2,1)S(1)}, u32[]{:S(2)}, u32[]{:S(2)}) async-start(bf16[8,2,24,2048]{3,2,1,0:T(8,128)(2,1)} %copy.53), calls=%async_computation | async-start | bytes 3145728 | tf_op jit(solution)/shard_map/while/body/eval_jaxpr/all_to_all | solution.py:74
  163.7 23.3 %collective-permute-start.2 = (bf16[1,1,2,24,2048]{4,3,2,1,0:T(8,128)(2,1)S(1)}, bf16[1,1,2,24,2048]{4,3,2,1,0:T(8,128)(2,1)}, u32[]{:S(2)}, u32[]{:S(2)}) collective-permute-start(bf16[1,1,2,24,2048]{4,3,2,1,0:T(8,128)(2,1)S(1)} %get-tuple-element.529), channel_id=1, source_target_pairs={{0,3},{1,4},{2,5},{3,6},{4,7},{5,0},{6,1},{7,2},{8,11},{9,12},{10,... | collective-permute-start | bytes 589832 | tf_op jit(solution)/shard_map/while/body/eval_jaxpr/ppermute | solution.py:27
  164.8 23.0 %collective-permute-start.3 = (bf16[1,1,2,24,2048]{4,3,2,1,0:T(8,128)(2,1)S(1)}, bf16[1,1,2,24,2048]{4,3,2,1,0:T(8,128)(2,1)S(1)}, u32[]{:S(2)}, u32[]{:S(2)}) collective-permute-start(bf16[1,1,2,24,2048]{4,3,2,1,0:T(8,128)(2,1)S(1)} %get-tuple-element.530), channel_id=1, source_target_pairs={{0,4},{1,5},{2,6},{3,7},{4,0},{5,1},{6,2},{7,3},{8,12},{9,13},{10,... | collective-permute-start | bytes 589832 | tf_op jit(solution)/shard_map/while/body/eval_jaxpr/ppermute | solution.py:27
  202.5 50.9 %all-to-all-start = ((bf16[8,2,24,2048]{3,2,1,0:T(8,128)(2,1)}), bf16[8,2,24,2048]{3,2,1,0:T(8,128)(2,1)S(1)}, u32[]{:S(2)}, u32[]{:S(2)}) async-start(bf16[8,2,24,2048]{3,2,1,0:T(8,128)(2,1)} %copy.53), calls=%async_computation | async-start | bytes 3145728 | tf_op jit(solution)/shard_map/while/body/eval_jaxpr/all_to_all | solution.py:74
  294.5 23.5 %collective-permute-start.2 = (bf16[1,1,2,24,2048]{4,3,2,1,0:T(8,128)(2,1)S(1)}, bf16[1,1,2,24,2048]{4,3,2,1,0:T(8,128)(2,1)}, u32[]{:S(2)}, u32[]{:S(2)}) collective-permute-start(bf16[1,1,2,24,2048]{4,3,2,1,0:T(8,128)(2,1)S(1)} %get-tuple-element.529), channel_id=1, source_target_pairs={{0,3},{1,4},{2,5},{3,6},{4,7},{5,0},{6,1},{7,2},{8,11},{9,12},{10,... | collective-permute-start | bytes 589832 | tf_op jit(solution)/shard_map/while/body/eval_jaxpr/ppermute | solution.py:27
  296.6 22.3 %collective-permute-start.3 = (bf16[1,1,2,24,2048]{4,3,2,1,0:T(8,128)(2,1)S(1)}, bf16[1,1,2,24,2048]{4,3,2,1,0:T(8,128)(2,1)S(1)}, u32[]{:S(2)}, u32[]{:S(2)}) collective-permute-start(bf16[1,1,2,24,2048]{4,3,2,1,0:T(8,128)(2,1)S(1)} %get-tuple-element.530), channel_id=1, source_target_pairs={{0,4},{1,5},{2,6},{3,7},{4,0},{5,1},{6,2},{7,3},{8,12},{9,13},{10,... | collective-permute-start | bytes 589832 | tf_op jit(solution)/shard_map/while/body/eval_jaxpr/ppermute | solution.py:27
  333.6 51.1 %all-to-all-start = ((bf16[8,2,24,2048]{3,2,1,0:T(8,128)(2,1)}), bf16[8,2,24,2048]{3,2,1,0:T(8,128)(2,1)S(1)}, u32[]{:S(2)}, u32[]{:S(2)}) async-start(bf16[8,2,24,2048]{3,2,1,0:T(8,128)(2,1)} %copy.53), calls=%async_computation | async-start | bytes 3145728 | tf_op jit(solution)/shard_map/while/body/eval_jaxpr/all_to_all | solution.py:74
  425.5 23.8 %collective-permute-start.2 = (bf16[1,1,2,24,2048]{4,3,2,1,0:T(8,128)(2,1)S(1)}, bf16[1,1,2,24,2048]{4,3,2,1,0:T(8,128)(2,1)}, u32[]{:S(2)}, u32[]{:S(2)}) collective-permute-start(bf16[1,1,2,24,2048]{4,3,2,1,0:T(8,128)(2,1)S(1)} %get-tuple-element.529), channel_id=1, source_target_pairs={{0,3},{1,4},{2,5},{3,6},{4,7},{5,0},{6,1},{7,2},{8,11},{9,12},{10,... | collective-permute-start | bytes 589832 | tf_op jit(solution)/shard_map/while/body/eval_jaxpr/ppermute | solution.py:27
  427.7 22.6 %collective-permute-start.3 = (bf16[1,1,2,24,2048]{4,3,2,1,0:T(8,128)(2,1)S(1)}, bf16[1,1,2,24,2048]{4,3,2,1,0:T(8,128)(2,1)S(1)}, u32[]{:S(2)}, u32[]{:S(2)}) collective-permute-start(bf16[1,1,2,24,2048]{4,3,2,1,0:T(8,128)(2,1)S(1)} %get-tuple-element.530), channel_id=1, source_target_pairs={{0,4},{1,5},{2,6},{3,7},{4,0},{5,1},{6,2},{7,3},{8,12},{9,13},{10,... | collective-permute-start | bytes 589832 | tf_op jit(solution)/shard_map/while/body/eval_jaxpr/ppermute | solution.py:27
  464.8 51.1 %all-to-all-start = ((bf16[8,2,24,2048]{3,2,1,0:T(8,128)(2,1)}), bf16[8,2,24,2048]{3,2,1,0:T(8,128)(2,1)S(1)}, u32[]{:S(2)}, u32[]{:S(2)}) async-start(bf16[8,2,24,2048]{3,2,1,0:T(8,128)(2,1)} %copy.53), calls=%async_computation | async-start | bytes 3145728 | tf_op jit(solution)/shard_map/while/body/eval_jaxpr/all_to_all | solution.py:74
  556.4 24.2 %collective-permute-start.2 = (bf16[1,1,2,24,2048]{4,3,2,1,0:T(8,128)(2,1)S(1)}, bf16[1,1,2,24,2048]{4,3,2,1,0:T(8,128)(2,1)}, u32[]{:S(2)}, u32[]{:S(2)}) collective-permute-start(bf16[1,1,2,24,2048]{4,3,2,1,0:T(8,128)(2,1)S(1)} %get-tuple-element.529), channel_id=1, source_target_pairs={{0,3},{1,4},{2,5},{3,6},{4,7},{5,0},{6,1},{7,2},{8,11},{9,12},{10,... | collective-permute-start | bytes 589832 | tf_op jit(solution)/shard_map/while/body/eval_jaxpr/ppermute | solution.py:27
  558.7 22.9 %collective-permute-start.3 = (bf16[1,1,2,24,2048]{4,3,2,1,0:T(8,128)(2,1)S(1)}, bf16[1,1,2,24,2048]{4,3,2,1,0:T(8,128)(2,1)S(1)}, u32[]{:S(2)}, u32[]{:S(2)}) collective-permute-start(bf16[1,1,2,24,2048]{4,3,2,1,0:T(8,128)(2,1)S(1)} %get-tuple-element.530), channel_id=1, source_target_pairs={{0,4},{1,5},{2,6},{3,7},{4,0},{5,1},{6,2},{7,3},{8,12},{9,13},{10,... | collective-permute-start | bytes 589832 | tf_op jit(solution)/shard_map/while/body/eval_jaxpr/ppermute | solution.py:27
  596.2 51.1 %all-to-all-start = ((bf16[8,2,24,2048]{3,2,1,0:T(8,128)(2,1)}), bf16[8,2,24,2048]{3,2,1,0:T(8,128)(2,1)S(1)}, u32[]{:S(2)}, u32[]{:S(2)}) async-start(bf16[8,2,24,2048]{3,2,1,0:T(8,128)(2,1)} %copy.53), calls=%async_computation | async-start | bytes 3145728 | tf_op jit(solution)/shard_map/while/body/eval_jaxpr/all_to_all | solution.py:74
  687.4 24.6 %collective-permute-start.2 = (bf16[1,1,2,24,2048]{4,3,2,1,0:T(8,128)(2,1)S(1)}, bf16[1,1,2,24,2048]{4,3,2,1,0:T(8,128)(2,1)}, u32[]{:S(2)}, u32[]{:S(2)}) collective-permute-start(bf16[1,1,2,24,2048]{4,3,2,1,0:T(8,128)(2,1)S(1)} %get-tuple-element.529), channel_id=1, source_target_pairs={{0,3},{1,4},{2,5},{3,6},{4,7},{5,0},{6,1},{7,2},{8,11},{9,12},{10,... | collective-permute-start | bytes 589832 | tf_op jit(solution)/shard_map/while/body/eval_jaxpr/ppermute | solution.py:27
  689.6 23.3 %collective-permute-start.3 = (bf16[1,1,2,24,2048]{4,3,2,1,0:T(8,128)(2,1)S(1)}, bf16[1,1,2,24,2048]{4,3,2,1,0:T(8,128)(2,1)S(1)}, u32[]{:S(2)}, u32[]{:S(2)}) collective-permute-start(bf16[1,1,2,24,2048]{4,3,2,1,0:T(8,128)(2,1)S(1)} %get-tuple-element.530), channel_id=1, source_target_pairs={{0,4},{1,5},{2,6},{3,7},{4,0},{5,1},{6,2},{7,3},{8,12},{9,13},{10,... | collective-permute-start | bytes 589832 | tf_op jit(solution)/shard_map/while/body/eval_jaxpr/ppermute | solution.py:27
  690.7 22.2 %collective-permute-start.4 = (bf16[1,1,2,24,2048]{4,3,2,1,0:T(8,128)(2,1)S(1)}, bf16[1,1,2,24,2048]{4,3,2,1,0:T(8,128)(2,1)S(1)}, u32[]{:S(2)}, u32[]{:S(2)}) collective-permute-start(bf16[1,1,2,24,2048]{4,3,2,1,0:T(8,128)(2,1)S(1)} %get-tuple-element.531), channel_id=1, source_target_pairs={{0,5},{1,6},{2,7},{3,0},{4,1},{5,2},{6,3},{7,4},{8,13},{9,14},{10,... | collective-permute-start | bytes 589832 | tf_op jit(solution)/shard_map/while/body/eval_jaxpr/ppermute | solution.py:27
  727.5 51.0 %all-to-all-start = ((bf16[8,2,24,2048]{3,2,1,0:T(8,128)(2,1)}), bf16[8,2,24,2048]{3,2,1,0:T(8,128)(2,1)S(1)}, u32[]{:S(2)}, u32[]{:S(2)}) async-start(bf16[8,2,24,2048]{3,2,1,0:T(8,128)(2,1)} %copy.53), calls=%async_computation | async-start | bytes 3145728 | tf_op jit(solution)/shard_map/while/body/eval_jaxpr/all_to_all | solution.py:74
  818.3 24.9 %collective-permute-start.2 = (bf16[1,1,2,24,2048]{4,3,2,1,0:T(8,128)(2,1)S(1)}, bf16[1,1,2,24,2048]{4,3,2,1,0:T(8,128)(2,1)}, u32[]{:S(2)}, u32[]{:S(2)}) collective-permute-start(bf16[1,1,2,24,2048]{4,3,2,1,0:T(8,128)(2,1)S(1)} %get-tuple-element.529), channel_id=1, source_target_pairs={{0,3},{1,4},{2,5},{3,6},{4,7},{5,0},{6,1},{7,2},{8,11},{9,12},{10,... | collective-permute-start | bytes 589832 | tf_op jit(solution)/shard_map/while/body/eval_jaxpr/ppermute | solution.py:27
  820.7 23.5 %collective-permute-start.3 = (bf16[1,1,2,24,2048]{4,3,2,1,0:T(8,128)(2,1)S(1)}, bf16[1,1,2,24,2048]{4,3,2,1,0:T(8,128)(2,1)S(1)}, u32[]{:S(2)}, u32[]{:S(2)}) collective-permute-start(bf16[1,1,2,24,2048]{4,3,2,1,0:T(8,128)(2,1)S(1)} %get-tuple-element.530), channel_id=1, source_target_pairs={{0,4},{1,5},{2,6},{3,7},{4,0},{5,1},{6,2},{7,3},{8,12},{9,13},{10,... | collective-permute-start | bytes 589832 | tf_op jit(solution)/shard_map/while/body/eval_jaxpr/ppermute | solution.py:27
  821.6 22.6 %collective-permute-start.4 = (bf16[1,1,2,24,2048]{4,3,2,1,0:T(8,128)(2,1)S(1)}, bf16[1,1,2,24,2048]{4,3,2,1,0:T(8,128)(2,1)S(1)}, u32[]{:S(2)}, u32[]{:S(2)}) collective-permute-start(bf16[1,1,2,24,2048]{4,3,2,1,0:T(8,128)(2,1)S(1)} %get-tuple-element.531), channel_id=1, source_target_pairs={{0,5},{1,6},{2,7},{3,0},{4,1},{5,2},{6,3},{7,4},{8,13},{9,14},{10,... | collective-permute-start | bytes 589832 | tf_op jit(solution)/shard_map/while/body/eval_jaxpr/ppermute | solution.py:27
  858.8 50.9 %all-to-all-start = ((bf16[8,2,24,2048]{3,2,1,0:T(8,128)(2,1)}), bf16[8,2,24,2048]{3,2,1,0:T(8,128)(2,1)S(1)}, u32[]{:S(2)}, u32[]{:S(2)}) async-start(bf16[8,2,24,2048]{3,2,1,0:T(8,128)(2,1)} %copy.53), calls=%async_computation | async-start | bytes 3145728 | tf_op jit(solution)/shard_map/while/body/eval_jaxpr/all_to_all | solution.py:74
  (46 other events, 589.7 us)
